TPU v7x, 32 devices: a whole 2x2x4 slice. The times are simulated.
32 devices in a mesh: section: 4 (over y, core), sim: 8 (over z, x).
Axes of the slice: x: 2, y: 2, z: 4, core: 2. Of those that a mesh axis runs over, the one named last changes fastest.
Arguments:
- state: float32 [128, 64, 8192], P('section', None, 'sim'), may hold values from -60 to 60
- owner: int32 [128, 1], P('section'), may hold values from 0 to 7; in each aligned block of 32 rows (0 to 31, 32 to 63, ...) at most 8 rows name the same one
- counts: int32 [128], P('section'), may hold values from 2048 to 8192
Outputs:
- slab_mean: float32 [128, 64], P('section')
- slab_cov: float32 [128, 4096], P('section', 'sim')
- group_cov: float32 [32, 4096], P(('section', 'sim'))
- global_mean: float32 [64], replicated
- global_cov: float32 [64, 64], replicated
Inputs may be any that keep to these rules, and one draw needn't show every extreme that they name: Among the 32 slabs of one group, no owner is named by more than 8 slabs, and one owner is named by exactly 8 slabs in some or all groups.
All inputs are finite; a program needn't handle non-finite values.
Results may differ from a plain program's by a relative error of at most 0.0003.
Values sent between devices are 32-bit elements; how exact they have to be, the bound alone decides.
A program may use at most 64 MiB of HBM per device.

v0:
```python
import jax
import jax.numpy as jnp
from jax import lax
from jax.sharding import PartitionSpec as P


def slot_payload(number, mean, comoment, capacity, n_sim, width):
    slot_cov = comoment / jnp.maximum(number - 1.0, 1.0)[:, None]
    cov_parts = slot_cov.reshape(capacity, n_sim, width * width // n_sim)
    mean_copies = jnp.broadcast_to(mean[:, None, :], (capacity, n_sim, width))
    return (cov_parts, mean_copies)


def owner_stats(number, mean, comoment):
    high = lax.Precision.HIGHEST
    width = mean.shape[1]
    group_count = jnp.sum(number)
    group_mean = jnp.sum(number[:, None] * mean, axis=0) / jnp.maximum(group_count, 1.0)
    offset = mean - group_mean[None, :]
    group_co = jnp.sum(comoment, axis=0) + jnp.einsum(
        "k,kv,kw->vw", number, offset, offset, precision=high
    ).reshape(width * width)
    return (group_count, group_mean, group_co)


def local(state, owner, counts):
    high = lax.Precision.HIGHEST
    slab_here, width, cells_dev = state.shape
    n_sim = lax.axis_size("sim")
    my_index = lax.axis_index("sim")
    capacity = 2 * slab_here // n_sim
    slots = n_sim * capacity
    target = owner[:, 0]
    order = jnp.arange(slab_here, dtype=jnp.int32)
    earlier = (target[:, None] == target[None, :]) & (order[None, :] < order[:, None])
    rank = jnp.sum(earlier.astype(jnp.int32), axis=1)
    slot_of = target * capacity + rank
    match = slot_of[:, None] == jnp.arange(slots, dtype=jnp.int32)[None, :]
    filled = jnp.any(match, axis=0)
    source_slab = jnp.sum(jnp.where(match, order[:, None], 0), axis=0)
    tile_start = my_index * cells_dev
    tile_count = jnp.clip(counts - tile_start, 0, cells_dev).astype(jnp.float32)
    live = jnp.arange(cells_dev, dtype=jnp.int32)[None, :] + tile_start < counts[:, None]
    tile_mean = (
        jnp.sum(jnp.where(live[:, None, :], state, 0.0), axis=2)
        / jnp.maximum(tile_count, 1.0)[:, None]
    )
    centered = jnp.where(live[:, None, :], state - tile_mean[:, :, None], 0.0)
    tile_co = jnp.einsum("svc,swc->svw", centered, centered, precision=high).reshape(
        slab_here, width * width
    )
    send_mean = jnp.where(filled[:, None], tile_mean[source_slab], 0.0).reshape(
        n_sim, capacity, width
    )
    send_co = jnp.where(filled[:, None], tile_co[source_slab], 0.0).reshape(
        n_sim, capacity, width * width
    )
    send_count = jnp.where(filled, tile_count[source_slab], 0.0).reshape(n_sim, capacity)
    means = lax.all_to_all(send_mean, "sim", split_axis=0, concat_axis=0, tiled=True)
    comoms = lax.all_to_all(send_co, "sim", split_axis=0, concat_axis=0, tiled=True)
    amounts = lax.all_to_all(send_count, "sim", split_axis=0, concat_axis=0, tiled=True)
    number = jnp.sum(amounts, axis=0)
    mean = jnp.sum(amounts[:, :, None] * means, axis=0) / jnp.maximum(number, 1.0)[:, None]
    offset = means - mean[None, :, :]
    extra = jnp.einsum("ik,ikv,ikw->kvw", amounts, offset, offset, precision=high)
    number, mean, comoment = (
        number,
        mean,
        jnp.sum(comoms, axis=0) + extra.reshape(number.shape[0], width * width),
    )
    cov_parts, mean_copies = slot_payload(number, mean, comoment, capacity, n_sim, width)
    back_cov, back_mean = (
        lax.all_to_all(cov_parts, "sim", split_axis=1, concat_axis=0, tiled=True),
        lax.all_to_all(mean_copies, "sim", split_axis=1, concat_axis=0, tiled=True),
    )
    slab_cov = back_cov[slot_of, 0]
    slab_mean = back_mean[slot_of, 0]
    group_count, group_mean, group_co = owner_stats(number, mean, comoment)
    group_cov = (group_co / jnp.maximum(group_count - 1.0, 1.0))[None, :]
    total, weighted = lax.psum((group_count, group_count * group_mean), ("section", "sim"))
    global_mean = weighted / total
    gap = group_mean - global_mean
    spread = lax.psum(group_co + group_count * jnp.outer(gap, gap).reshape(-1), ("section", "sim"))
    global_cov = (spread / (total - 1.0)).reshape(width, width)
    return (slab_mean, slab_cov, group_cov, global_mean, global_cov)


def solution(mesh):
    return jax.shard_map(
        local,
        mesh=mesh,
        in_specs=(P("section", None, "sim"), P("section", None), P("section")),
        out_specs=(P("section", None), P("section", "sim"), P(("section", "sim"), None), P(), P()),
        check_vma=False,
    )
```

profile of v0, /device:TPU:0, one launch (start us, length us, event | category | flops | bytes accessed | tf_op | source)
XLA Modules:
  0.0 160.8 jit_solution(15916009984353185825)
XLA Ops:
  0.6 0.9 convert_reduce_fusion
  1.5 0.7 fusion.19
  2.2 0.1 fusion.10
  2.3 0.1 select_reduce_fusion.1
  2.4 0.7 broadcast_maximum_fusion.1
  3.1 0.8 gather_fusion
  3.9 0.7 select_n.56
  4.5 7.3 %all-to-all-start = ((f32[8,1,8]{2,1,0:T(1,128)}), f32[8,1,8]{2,1,0:T(1,128)S(1)}, u32[]{:S(2)}, u32[]{:S(2)}) async-start(f32[8,1,8]{2,1,0:T(1,128)} %bitcast.5), calls=%async_computation | async-start | bytes 8192 | tf_op jit(solution)/shard_map/all_to_all | solution.py:61
  11.8 0.1 broadcast_in_dim.63
  11.9 0.7 broadcast_compare_fusion
  12.7 4.1 %select_reduce_fusion = f32[32,64]{1,0:T(8,128)S(1)} fusion(f32[32,64,1024]{2,1,0:T(8,128)} %param.3, pred[32,1024]{1,0:T(8,128)(4,1)S(1)} %broadcast_compare_fusion), kind=kLoop, calls=%fused_computation.8 | loop fusion | flops 4192256 | bytes 8429568 | tf_op jit(solution)/shard_map/reduce_sum | solution.py:45
  16.8 0.1 broadcast_divide_fusion.2
  16.9 0.6 gather_fusion.1
  17.5 14.9 %fusion = f32[32,64,64]{2,1,0:T(8,128)S(1)} fusion(f32[32,64,1024]{2,1,0:T(8,128)} %param.3, f32[32,64]{1,0:T(8,128)S(1)} %broadcast_divide_fusion.2, pred[32,1024]{1,0:T(8,128)(4,1)S(1)} %broadcast_compare_fusion), kind=kOutput, calls=%fused_computation.5 | convolution fusion | flops 1614807040 | bytes 8953856 | tf_op jit(solution)/shard_map/svc,swc->svw/dot_general | solution.py:49
  32.4 0.1 bitcast_select_fusion.1
  32.5 0.7 reshape.244
  33.2 0.4 reshape.205
  33.5 0.9 gather_fusion.3
  34.5 6.0 %all-to-all-start.1 = ((f32[8,1,512]{2,1,0:T(1,128)}), f32[8,1,512]{2,1,0:T(1,128)S(1)}, u32[]{:S(2)}, u32[]{:S(2)}) async-start(f32[8,1,512]{2,1,0:T(1,128)} %reshape.244), calls=%async_computation.1 | async-start | bytes 32768 | tf_op jit(solution)/shard_map/all_to_all | solution.py:59
  40.5 0.6 fusion.22
  41.1 6.0 %all-to-all-done.1 = f32[8,1,512]{2,1,0:T(1,128)S(1)} async-done(((f32[8,1,512]{2,1,0:T(1,128)}), f32[8,1,512]{2,1,0:T(1,128)S(1)}, u32[]{:S(2)}, u32[]{:S(2)}) %all-to-all-start.1) | async-done | bytes 16416 | tf_op jit(solution)/shard_map/all_to_all | solution.py:59
  47.1 0.5 broadcast.202
  47.6 0.7 reduce.4
  48.3 0.1 reshape.245
  48.3 0.1 multiply_reduce_fusion
  48.4 0.1 multiply_reduce_fusion.1
  48.5 0.7 reshape.246
  49.2 3.3 %all-to-all-start.2 = ((f32[8,1,512]{2,1,0:T(1,128)}), f32[8,1,512]{2,1,0:T(1,128)S(1)}, u32[]{:S(2)}, u32[]{:S(2)}) async-start(f32[8,1,512]{2,1,0:T(1,128)} %reshape.246), calls=%async_computation.2 | async-start | bytes 32768 | tf_op jit(solution)/shard_map/all_to_all | solution.py:74
  52.6 1.1 bitcast_select_fusion
  53.7 5.4 %all-to-all-done.2 = f32[8,1,512]{2,1,0:T(1,128)S(1)} async-done(((f32[8,1,512]{2,1,0:T(1,128)}), f32[8,1,512]{2,1,0:T(1,128)S(1)}, u32[]{:S(2)}, u32[]{:S(2)}) %all-to-all-start.2) | async-done | bytes 16416 | tf_op jit(solution)/shard_map/all_to_all | solution.py:74
  59.1 3.6 %all-to-all-start.3 = ((f32[8,8,4096]{2,1,0:T(8,128)}), f32[8,8,4096]{2,1,0:T(8,128)S(1)}, u32[]{:S(2)}, u32[]{:S(2)}) async-start(f32[8,8,4096]{2,1,0:T(8,128)} %bitcast_select_fusion), calls=%async_computation.3 | async-start | bytes 2097152 | tf_op jit(solution)/shard_map/all_to_all | solution.py:60
  63.9 0.7 broadcast_multiply_fusion.1
  64.6 41.6 %all-reduce.1 = (f32[64]{0:T(128)S(1)}, f32[]{:T(128)}) all-reduce(f32[64]{0:T(128)S(1)} %get-tuple-element.11, f32[]{:T(128)} %get-tuple-element.5), channel_id=1, replica_groups=mesh['section'=4,'sim'=8] {'section','sim'}, use_global_device_ids=true, to_apply=%region_10.11 | all-reduce | flops 65 | bytes 520 | tf_op jit(solution)/shard_map/psum | solution.py:80
  106.8 1.2 fusion.23
  108.1 0.7 reduce.5
  108.8 0.1 reshape.247
  108.8 1.2 gather_fusion.2
  110.1 0.1 reduce_sum.98
  110.2 0.6 add_reduce_fusion
  110.8 0.1 reshape.206
  110.9 0.7 fusion.6
  111.7 5.3 %all-to-all-start.4 = ((f32[8,8,512]{2,0,1:T(8,128)}), f32[8,8,512]{2,0,1:T(8,128)S(1)}, u32[]{:S(2)}, u32[]{:S(2)}) async-start(f32[8,8,512]{2,0,1:T(8,128)} %fusion.6), calls=%async_computation.4 | async-start | bytes 262144 | tf_op jit(solution)/shard_map/all_to_all | solution.py:73
  117.0 1.0 multiply_add_fusion
  117.9 0.7 div.85
  118.7 40.0 %psum.23 = f32[4096]{0:T(1024)S(1)} all-reduce(f32[4096]{0:T(1024)S(1)} %add.82), channel_id=1, replica_groups=mesh['section'=4,'sim'=8] {'section','sim'}, use_global_device_ids=true, to_apply=%region_12.13 | all-reduce | flops 4096 | bytes 32768 | tf_op jit(solution)/shard_map/psum | solution.py:83
  158.7 0.7 reshape.207
  159.4 0.1 all_to_all.46
  159.6 1.2 gather_fusion.4
  (13 shorter events, 0.2 us)
Async XLA Ops:
  4.5 29.9 %all-to-all-start = ((f32[8,1,8]{2,1,0:T(1,128)}), f32[8,1,8]{2,1,0:T(1,128)S(1)}, u32[]{:S(2)}, u32[]{:S(2)}) async-start(f32[8,1,8]{2,1,0:T(1,128)} %bitcast.5), calls=%async_computation | async-start | bytes 8192 | tf_op jit(solution)/shard_map/all_to_all | solution.py:61
  34.5 12.6 %all-to-all-start.1 = ((f32[8,1,512]{2,1,0:T(1,128)}), f32[8,1,512]{2,1,0:T(1,128)S(1)}, u32[]{:S(2)}, u32[]{:S(2)}) async-start(f32[8,1,512]{2,1,0:T(1,128)} %reshape.244), calls=%async_computation.1 | async-start | bytes 32768 | tf_op jit(solution)/shard_map/all_to_all | solution.py:59
  49.2 9.9 %all-to-all-start.2 = ((f32[8,1,512]{2,1,0:T(1,128)}), f32[8,1,512]{2,1,0:T(1,128)S(1)}, u32[]{:S(2)}, u32[]{:S(2)}) async-start(f32[8,1,512]{2,1,0:T(1,128)} %reshape.246), calls=%async_computation.2 | async-start | bytes 32768 | tf_op jit(solution)/shard_map/all_to_all | solution.py:74
  59.1 51.0 %all-to-all-start.3 = ((f32[8,8,4096]{2,1,0:T(8,128)}), f32[8,8,4096]{2,1,0:T(8,128)S(1)}, u32[]{:S(2)}, u32[]{:S(2)}) async-start(f32[8,8,4096]{2,1,0:T(8,128)} %bitcast_select_fusion), calls=%async_computation.3 | async-start | bytes 2097152 | tf_op jit(solution)/shard_map/all_to_all | solution.py:60
  111.7 47.8 %all-to-all-start.4 = ((f32[8,8,512]{2,0,1:T(8,128)}), f32[8,8,512]{2,0,1:T(8,128)S(1)}, u32[]{:S(2)}, u32[]{:S(2)}) async-start(f32[8,8,512]{2,0,1:T(8,128)} %fusion.6), calls=%async_computation.4 | async-start | bytes 262144 | tf_op jit(solution)/shard_map/all_to_all | solution.py:73
where the time goes:
time: 162 us; the launch traced here: 161 us
  blocking collectives  81.6 us (50%)
  starting transfers between devices  25.5 us (16%)
  matrix products  16.5 us (10%)
  other arithmetic  13.4 us (8%)
  waiting for transfers between devices  11.3 us (7%)
  local copies, waits for them, and re-layouts  9.73 us (6%)
  between operations  2.71 us (2%)
    psum x1, blocking collectives, local(): lax.psum((group_count, group_count * group_mean), ('section', 'sim'))  41.6 us
    psum x1, blocking collectives, local(): lax.psum(group_co + group_count * jnp.outer(gap, gap).reshape(-1), ('sect...  40 us
    dot_general x1, matrix products, local(): jnp.einsum('svc,swc->svw', centered, centered, precision=high)  14.9 us
    all_to_all x1, starting transfers between devices, local(): lax.all_to_all(send_count, 'sim', split_axis=0, concat_axis=0, tiled=True)  7.28 us
    all_to_all x1, starting transfers between devices, local(): lax.all_to_all(send_mean, 'sim', split_axis=0, concat_axis=0, tiled=True)  6.01 us
    all_to_all x1, waiting for transfers between devices, local(): lax.all_to_all(send_mean, 'sim', split_axis=0, concat_axis=0, tiled=True)  5.96 us
    all_to_all x1, waiting for transfers between devices, local(): lax.all_to_all(mean_copies, 'sim', split_axis=1, concat_axis=0, tiled=True)  5.37 us
    all_to_all x1, starting transfers between devices, local(): lax.all_to_all(cov_parts, 'sim', split_axis=1, concat_axis=0, tiled=True)  5.31 us
  transfers between devices with their start and end apart: 5, of which 2 were waited for; matrix products, arithmetic and copies ran while one was open for 19% of the time, Pallas kernels for 0%

commit v1 on v0

--- a/solution.py
+++ b/solution.py
@@ -80,7 +80,8 @@
     total, weighted = lax.psum((group_count, group_count * group_mean), ("section", "sim"))
     global_mean = weighted / total
     gap = group_mean - global_mean
-    spread = lax.psum(group_co + group_count * jnp.outer(gap, gap).reshape(-1), ("section", "sim"))
+    inner = lax.psum(group_co + group_count * jnp.outer(gap, gap).reshape(-1), "sim")
+    spread = lax.psum(inner, "section")
     global_cov = (spread / (total - 1.0)).reshape(width, width)
     return (slab_mean, slab_cov, group_cov, global_mean, global_cov)
 

time: 162 us -> 169 us (1.043)
  blocking collectives: 81.6 us -> 89.3 us
    psum x1 -> x2, blocking collectives: 40 us -> 47.7 us  [the longest x1 37.5 us: local(): lax.psum(group_co + group_count * jnp.outer(gap, gap).reshape(-1), 'sim')]
  transfers between devices with their start and end apart: 5 -> 5, of which waited for: 2 -> 2; matrix products, arithmetic and copies ran while one was open for 19% -> 18% of each run, Pallas kernels for 0% -> 0%
where the time goes in v1:
time: 169 us; the launch traced here: 168 us
  blocking collectives  89.3 us (53%)
  starting transfers between devices  25.5 us (15%)
  matrix products  16.5 us (10%)
  other arithmetic  13.4 us (8%)
  waiting for transfers between devices  11.3 us (7%)
  local copies, waits for them, and re-layouts  9.73 us (6%)
  between operations  2.71 us (2%)
    psum x1, blocking collectives, local(): lax.psum((group_count, group_count * group_mean), ('section', 'sim'))  41.6 us
    psum x1, blocking collectives, local(): lax.psum(group_co + group_count * jnp.outer(gap, gap).reshape(-1), 'sim')  37.5 us
    dot_general x1, matrix products, local(): jnp.einsum('svc,swc->svw', centered, centered, precision=high)  14.9 us
    psum x1, blocking collectives, local(): spread = lax.psum(inner, 'section')  10.1 us
    all_to_all x1, starting transfers between devices, local(): lax.all_to_all(send_count, 'sim', split_axis=0, concat_axis=0, tiled=True)  7.28 us
    all_to_all x1, starting transfers between devices, local(): lax.all_to_all(send_mean, 'sim', split_axis=0, concat_axis=0, tiled=True)  6.01 us
    all_to_all x1, waiting for transfers between devices, local(): lax.all_to_all(send_mean, 'sim', split_axis=0, concat_axis=0, tiled=True)  5.96 us
    all_to_all x1, waiting for transfers between devices, local(): lax.all_to_all(mean_copies, 'sim', split_axis=1, concat_axis=0, tiled=True)  5.37 us
  transfers between devices with their start and end apart: 5, of which 2 were waited for; matrix products, arithmetic and copies ran while one was open for 18% of the time, Pallas kernels for 0%

profile of v1, /device:TPU:0, one launch (start us, length us, event | category | flops | bytes accessed | tf_op | source)
XLA Modules:
  0.0 168.5 jit_solution(14658935564518423849)
XLA Ops:
  0.6 0.9 convert_reduce_fusion
  1.5 0.7 fusion.19
  2.2 0.1 fusion.10
  2.3 0.1 select_reduce_fusion.1
  2.4 0.7 broadcast_maximum_fusion.1
  3.1 0.8 gather_fusion
  3.9 0.7 select_n.56
  4.5 7.3 %all-to-all-start = ((f32[8,1,8]{2,1,0:T(1,128)}), f32[8,1,8]{2,1,0:T(1,128)S(1)}, u32[]{:S(2)}, u32[]{:S(2)}) async-start(f32[8,1,8]{2,1,0:T(1,128)} %bitcast.5), calls=%async_computation | async-start | bytes 8192 | tf_op jit(solution)/shard_map/all_to_all | solution.py:61
  11.8 0.1 broadcast_in_dim.63
  11.9 0.7 broadcast_compare_fusion
  12.7 4.1 %select_reduce_fusion = f32[32,64]{1,0:T(8,128)S(1)} fusion(f32[32,64,1024]{2,1,0:T(8,128)} %param.3, pred[32,1024]{1,0:T(8,128)(4,1)S(1)} %broadcast_compare_fusion), kind=kLoop, calls=%fused_computation.8 | loop fusion | flops 4192256 | bytes 8429568 | tf_op jit(solution)/shard_map/reduce_sum | solution.py:45
  16.8 0.1 broadcast_divide_fusion.2
  16.9 0.6 gather_fusion.1
  17.5 14.9 %fusion = f32[32,64,64]{2,1,0:T(8,128)S(1)} fusion(f32[32,64,1024]{2,1,0:T(8,128)} %param.3, f32[32,64]{1,0:T(8,128)S(1)} %broadcast_divide_fusion.2, pred[32,1024]{1,0:T(8,128)(4,1)S(1)} %broadcast_compare_fusion), kind=kOutput, calls=%fused_computation.5 | convolution fusion | flops 1614807040 | bytes 8953856 | tf_op jit(solution)/shard_map/svc,swc->svw/dot_general | solution.py:49
  32.4 0.1 bitcast_select_fusion.1
  32.5 0.7 reshape.244
  33.2 0.4 reshape.205
  33.5 0.9 gather_fusion.3
  34.5 6.0 %all-to-all-start.1 = ((f32[8,1,512]{2,1,0:T(1,128)}), f32[8,1,512]{2,1,0:T(1,128)S(1)}, u32[]{:S(2)}, u32[]{:S(2)}) async-start(f32[8,1,512]{2,1,0:T(1,128)} %reshape.244), calls=%async_computation.1 | async-start | bytes 32768 | tf_op jit(solution)/shard_map/all_to_all | solution.py:59
  40.5 0.6 fusion.22
  41.1 6.0 %all-to-all-done.1 = f32[8,1,512]{2,1,0:T(1,128)S(1)} async-done(((f32[8,1,512]{2,1,0:T(1,128)}), f32[8,1,512]{2,1,0:T(1,128)S(1)}, u32[]{:S(2)}, u32[]{:S(2)}) %all-to-all-start.1) | async-done | bytes 16416 | tf_op jit(solution)/shard_map/all_to_all | solution.py:59
  47.1 0.5 broadcast.202
  47.6 0.7 reduce.4
  48.3 0.1 multiply_reduce_fusion
  48.4 0.1 multiply_reduce_fusion.1
  48.5 0.7 reshape.246
  49.2 3.3 %all-to-all-start.2 = ((f32[8,1,512]{2,1,0:T(1,128)}), f32[8,1,512]{2,1,0:T(1,128)S(1)}, u32[]{:S(2)}, u32[]{:S(2)}) async-start(f32[8,1,512]{2,1,0:T(1,128)} %reshape.246), calls=%async_computation.2 | async-start | bytes 32768 | tf_op jit(solution)/shard_map/all_to_all | solution.py:74
  52.6 1.1 bitcast_select_fusion
  53.7 5.4 %all-to-all-done.2 = f32[8,1,512]{2,1,0:T(1,128)S(1)} async-done(((f32[8,1,512]{2,1,0:T(1,128)}), f32[8,1,512]{2,1,0:T(1,128)S(1)}, u32[]{:S(2)}, u32[]{:S(2)}) %all-to-all-start.2) | async-done | bytes 16416 | tf_op jit(solution)/shard_map/all_to_all | solution.py:74
  59.1 3.6 %all-to-all-start.3 = ((f32[8,8,4096]{2,1,0:T(8,128)}), f32[8,8,4096]{2,1,0:T(8,128)S(1)}, u32[]{:S(2)}, u32[]{:S(2)}) async-start(f32[8,8,4096]{2,1,0:T(8,128)} %bitcast_select_fusion), calls=%async_computation.3 | async-start | bytes 2097152 | tf_op jit(solution)/shard_map/all_to_all | solution.py:60
  63.9 0.7 broadcast_multiply_fusion.1
  64.6 41.6 %all-reduce.1 = (f32[64]{0:T(128)S(1)}, f32[]{:T(128)}) all-reduce(f32[64]{0:T(128)S(1)} %get-tuple-element.11, f32[]{:T(128)} %get-tuple-element.5), channel_id=1, replica_groups=mesh['section'=4,'sim'=8] {'section','sim'}, use_global_device_ids=true, to_apply=%region_10.11 | all-reduce | flops 65 | bytes 520 | tf_op jit(solution)/shard_map/psum | solution.py:80
  106.8 1.2 fusion.23
  108.1 0.7 reduce.5
  108.8 0.1 reshape.247
  108.8 1.2 gather_fusion.2
  110.1 0.1 reduce_sum.98
  110.2 0.6 add_reduce_fusion
  110.8 0.1 reshape.206
  110.9 0.7 fusion.6
  111.7 5.3 %all-to-all-start.4 = ((f32[8,8,512]{2,0,1:T(8,128)}), f32[8,8,512]{2,0,1:T(8,128)S(1)}, u32[]{:S(2)}, u32[]{:S(2)}) async-start(f32[8,8,512]{2,0,1:T(8,128)} %fusion.6), calls=%async_computation.4 | async-start | bytes 262144 | tf_op jit(solution)/shard_map/all_to_all | solution.py:73
  117.0 1.0 multiply_add_fusion
  118.0 37.5 %psum.30 = f32[4096]{0:T(1024)S(1)} all-reduce(f32[4096]{0:T(1024)S(1)} %add.84), channel_id=1, replica_groups=mesh['section'=4,'sim'=8] {'sim'}, use_global_device_ids=true, to_apply=%region_12.13 | all-reduce | flops 4096 | bytes 32768 | tf_op jit(solution)/shard_map/psum | solution.py:83
  155.6 10.1 %psum.31 = f32[4096]{0:T(1024)S(1)} all-reduce(f32[4096]{0:T(1024)S(1)} %psum.30), channel_id=1, replica_groups=mesh['section'=4,'sim'=8] {'section'}, use_global_device_ids=true, to_apply=%region_13.14 | all-reduce | flops 4096 | bytes 32768 | tf_op jit(solution)/shard_map/psum | solution.py:84
  165.7 0.7 div.85
  166.4 0.7 reshape.207
  167.1 0.1 all_to_all.46
  167.2 1.2 gather_fusion.4
  (14 shorter events, 0.3 us)
Async XLA Ops:
  4.5 29.9 %all-to-all-start = ((f32[8,1,8]{2,1,0:T(1,128)}), f32[8,1,8]{2,1,0:T(1,128)S(1)}, u32[]{:S(2)}, u32[]{:S(2)}) async-start(f32[8,1,8]{2,1,0:T(1,128)} %bitcast.5), calls=%async_computation | async-start | bytes 8192 | tf_op jit(solution)/shard_map/all_to_all | solution.py:61
  34.5 12.6 %all-to-all-start.1 = ((f32[8,1,512]{2,1,0:T(1,128)}), f32[8,1,512]{2,1,0:T(1,128)S(1)}, u32[]{:S(2)}, u32[]{:S(2)}) async-start(f32[8,1,512]{2,1,0:T(1,128)} %reshape.244), calls=%async_computation.1 | async-start | bytes 32768 | tf_op jit(solution)/shard_map/all_to_all | solution.py:59
  49.2 9.9 %all-to-all-start.2 = ((f32[8,1,512]{2,1,0:T(1,128)}), f32[8,1,512]{2,1,0:T(1,128)S(1)}, u32[]{:S(2)}, u32[]{:S(2)}) async-start(f32[8,1,512]{2,1,0:T(1,128)} %reshape.246), calls=%async_computation.2 | async-start | bytes 32768 | tf_op jit(solution)/shard_map/all_to_all | solution.py:74
  59.1 51.0 %all-to-all-start.3 = ((f32[8,8,4096]{2,1,0:T(8,128)}), f32[8,8,4096]{2,1,0:T(8,128)S(1)}, u32[]{:S(2)}, u32[]{:S(2)}) async-start(f32[8,8,4096]{2,1,0:T(8,128)} %bitcast_select_fusion), calls=%async_computation.3 | async-start | bytes 2097152 | tf_op jit(solution)/shard_map/all_to_all | solution.py:60
  111.7 55.4 %all-to-all-start.4 = ((f32[8,8,512]{2,0,1:T(8,128)}), f32[8,8,512]{2,0,1:T(8,128)S(1)}, u32[]{:S(2)}, u32[]{:S(2)}) async-start(f32[8,8,512]{2,0,1:T(8,128)} %fusion.6), calls=%async_computation.4 | async-start | bytes 262144 | tf_op jit(solution)/shard_map/all_to_all | solution.py:73
